TPU v7x, 32 devices: a whole 2x2x4 slice. The times are simulated.
32 devices in a mesh: seq: 8 (over z, x), exp: 4 (over y, core).
Axes of the slice: x: 2, y: 2, z: 4, core: 2. Of those that a mesh axis runs over, the one named last changes fastest.
Arguments:
- tokens: bfloat16 [4, 1024, 4096], P('exp', 'seq'), may hold values from -6 to 6
- out_grad: bfloat16 [4, 1024, 4096], P('exp', 'seq'), may hold values from -0.59765625 to 0.59765625
- router_weight: bfloat16 [4096, 32], replicated, may hold values from -8 to 8
- gate_weight: bfloat16 [32, 4096, 768], P(('seq', 'exp')), may hold values from -0.09375 to 0.09375
- up_weight: bfloat16 [32, 4096, 768], P(('seq', 'exp')), may hold values from -0.09375 to 0.09375
- down_weight: bfloat16 [32, 768, 4096], P(('seq', 'exp')), may hold values from -0.21875 to 0.21875
- saved_gate: bfloat16 [32, 2048, 768], P(('seq', 'exp')), may hold values from -6 to 6
- saved_up: bfloat16 [32, 2048, 768], P(('seq', 'exp')), may hold values from -6 to 6
- expert_ids: int32 [4, 1024, 8], P('exp', 'seq'), may hold values from 0 to 31, as said below
- aux_weight: float32 [1], replicated, may hold values from 2 to 6
Outputs:
- token_grad: bfloat16 [4, 1024, 4096], P('exp', 'seq')
- combine_grad: float32 [4, 1024, 8], P('exp', 'seq')
- router_grad: float32 [4096, 32], P(('seq', 'exp'))
Inputs may be any that keep to these rules, and one draw needn't show every extreme that they name: `expert_ids`: among the rows of one device (128 tokens) each expert is named at most 64 times, and some expert exactly 64 times; a token's 8 experts differ.
All inputs are finite; a program needn't handle non-finite values.
Results may differ from a plain program's by a relative error of at most 0.013.
Values may be sent and summed in bfloat16 or wider, within the bound.
A program may use at most 192 MiB of HBM per device.

v0:
```python
import jax
import jax.numpy as jnp
from jax import lax
from jax.sharding import PartitionSpec as P


def expert_backward(grad_rows, gate_rows, w_gate, w_up, w_down, pre_gate, pre_up):
    upstream = jnp.einsum("rd,fd->rf", grad_rows, w_down, preferred_element_type=jnp.float32)
    first = pre_gate.astype(jnp.float32)
    second = pre_up.astype(jnp.float32)
    gate_sig = jax.nn.sigmoid(first)
    gate_act = first * gate_sig
    hidden = gate_act * second
    slot_combine = jnp.sum(upstream * hidden, axis=-1).astype(jnp.bfloat16)
    scaled = gate_rows.astype(jnp.float32)[:, None] * upstream
    grad_first = (scaled * second * gate_sig * (1.0 + first * (1.0 - gate_sig))).astype(
        jnp.bfloat16
    )
    grad_second = (scaled * gate_act).astype(jnp.bfloat16)
    back_rows = jnp.einsum("rf,df->rd", grad_first, w_gate, preferred_element_type=jnp.float32)
    back_rows = back_rows + jnp.einsum(
        "rf,df->rd", grad_second, w_up, preferred_element_type=jnp.float32
    )
    return (back_rows.astype(jnp.bfloat16), slot_combine)


def shards(
    tokens,
    out_grad,
    router_weight,
    gate_weight,
    up_weight,
    down_weight,
    saved_gate,
    saved_up,
    expert_ids,
    aux_weight,
):
    seq_size = lax.axis_size("seq")
    exp_size = lax.axis_size("exp")
    devices = seq_size * exp_size
    inputs = tokens[0]
    upstream_grad = out_grad[0]
    chosen_ids = expert_ids[0]
    tok_rows, top_count = chosen_ids.shape
    model_width = inputs.shape[1]
    experts = router_weight.shape[1]
    capacity = saved_gate.shape[1] // devices
    logits = jnp.dot(inputs, router_weight, preferred_element_type=jnp.float32)
    router_probs = jax.nn.softmax(logits, axis=-1)
    chosen = jnp.take_along_axis(router_probs, chosen_ids, axis=1)
    chosen_sum = jnp.sum(chosen, axis=1, keepdims=True)
    gate_vals = chosen / chosen_sum
    onehot = (
        chosen_ids.reshape(-1)[:, None] == jnp.arange(experts, dtype=jnp.int32)[None, :]
    ).astype(jnp.int32)
    rank_before = jnp.cumsum(onehot, axis=0) - onehot
    slot_pos = jnp.sum(rank_before * onehot, axis=1)
    slot_index = chosen_ids.reshape(-1) * capacity + slot_pos
    token_order = jnp.arange(tok_rows * top_count, dtype=jnp.int32) // top_count
    slot_token = (
        jnp.full((experts * capacity,), tok_rows, jnp.int32).at[slot_index].set(token_order)
    )
    grad_padded = jnp.concatenate(
        [upstream_grad, jnp.zeros((1, model_width), jnp.bfloat16)], axis=0
    )
    grad_slots = grad_padded[slot_token]
    gate_slots = (
        jnp.zeros((experts * capacity,), jnp.bfloat16)
        .at[slot_index]
        .set(gate_vals.reshape(-1).astype(jnp.bfloat16))
    )
    chosen_count = jnp.sum(onehot.reshape(tok_rows, top_count, experts), axis=1).astype(jnp.float32)
    local_counts = jnp.sum(chosen_count, axis=0)
    seq_counts = lax.psum(local_counts, "seq")
    recv_grad, recv_gate = (
        lax.all_to_all(
            grad_slots.reshape(experts, 1, capacity, model_width),
            ("seq", "exp"),
            split_axis=0,
            concat_axis=1,
            tiled=True,
        ),
        lax.all_to_all(
            gate_slots.reshape(experts, 1, capacity),
            ("seq", "exp"),
            split_axis=0,
            concat_axis=1,
            tiled=True,
        ),
    )
    back_rows, slot_combine = expert_backward(
        recv_grad.reshape(-1, model_width),
        recv_gate.reshape(-1),
        gate_weight[0],
        up_weight[0],
        down_weight[0],
        saved_gate[0],
        saved_up[0],
    )
    returned, combine_back = (
        lax.all_to_all(
            back_rows.reshape(1, devices, capacity, model_width),
            ("seq", "exp"),
            split_axis=1,
            concat_axis=0,
            tiled=True,
        ),
        lax.all_to_all(
            slot_combine.reshape(1, devices, capacity),
            ("seq", "exp"),
            split_axis=1,
            concat_axis=0,
            tiled=True,
        ),
    )
    returned_rows = returned.reshape(experts * capacity, model_width)
    expert_sum = jnp.sum(
        returned_rows[slot_index].reshape(tok_rows, top_count, model_width).astype(jnp.float32),
        axis=1,
    )
    combine_grad = (
        combine_back.reshape(-1)[slot_index].reshape(tok_rows, top_count).astype(jnp.float32)
    )
    prob_sel = (
        combine_grad - jnp.sum(gate_vals * combine_grad, axis=1, keepdims=True)
    ) / chosen_sum
    prob_grad = jnp.einsum(
        "tk,tke->te", prob_sel, onehot.reshape(tok_rows, top_count, experts).astype(jnp.float32)
    )
    fraction = experts * seq_counts / (top_count * tok_rows * seq_size)
    prob_grad = prob_grad + aux_weight[0] * fraction[None, :]
    dlogits = router_probs * (prob_grad - jnp.sum(router_probs * prob_grad, axis=1, keepdims=True))
    logit_grad = dlogits.astype(jnp.bfloat16)
    token_grad = expert_sum + jnp.einsum(
        "te,de->td", logit_grad, router_weight, preferred_element_type=jnp.float32
    )
    router_grad = lax.psum_scatter(
        jnp.einsum("td,te->de", inputs, logit_grad, preferred_element_type=jnp.float32),
        ("seq", "exp"),
        scatter_dimension=0,
        tiled=True,
    )
    return (token_grad.astype(jnp.bfloat16)[None], combine_grad[None], router_grad)


def solution(mesh):
    placed = (
        P("exp", "seq", None),
        P("exp", "seq", None),
        P(),
        P(("seq", "exp"), None, None),
        P(("seq", "exp"), None, None),
        P(("seq", "exp"), None, None),
        P(("seq", "exp"), None, None),
        P(("seq", "exp"), None, None),
        P("exp", "seq", None),
        P(),
    )
    return jax.shard_map(
        shards,
        mesh=mesh,
        in_specs=placed,
        out_specs=(P("exp", "seq", None), P("exp", "seq", None), P(("seq", "exp"), None)),
        check_vma=False,
    )
```

profile of v0, /device:TPU:0, one launch (start us, length us, event | category | flops | bytes accessed | tf_op | source)
XLA Modules:
  0.0 1073.2 jit_solution(6550109645006879006)
XLA Ops:
  7.2 0.0 copy-start
  7.2 0.9 copy.54
  8.1 0.1 eq.36
  8.1 0.1 eq.32
  8.2 0.7 broadcast_multiply_fusion
  8.9 0.7 fusion.39
  9.6 9.0 reduce-window.6
  18.7 0.1 slice.16
  18.8 0.1 copy.56
  18.9 0.1 copy.57
  19.0 0.1 broadcast_add_fusion
  19.1 0.1 copy.53
  19.2 0.1 mul.75
  19.3 1.4 fusion.47
  20.7 0.0 copy-start.3
  20.8 0.5 copy-done.3
  21.4 0.1 copy.58
  21.5 0.1 reshape.223
  21.5 0.0 copy-start.1
  21.6 7.0 gather_fusion.3
  28.6 0.1 reshape.226
  28.7 0.1 fusion.34
  28.8 0.1 div.42
  28.9 0.1 div.43
  29.1 7.6 scatter_custom_fusion
  36.7 0.7 reshape.249
  37.4 7.3 all-to-all-start
  44.7 4.3 scatter_custom_fusion.1
  49.1 0.1 concatenate.3
  49.2 14.3 %gather_fusion = bf16[2048,4096]{1,0:T(8,128)(2,1)} fusion(bf16[129,4096]{1,0:T(8,128)(2,1)S(1)} %concatenate.3, s32[2048]{0:T(1024)S(1)} %fusion.33), kind=kCustom, calls=%fused_computation | custom fusion | bytes 33562624 | tf_op jit(solution)/shard_map/gather | solution.py:67
  63.5 0.0 all-to-all-done
  63.5 6.4 all-to-all-start.1
  69.9 4.7 copy.63
  74.6 4.7 copy.62
  79.4 0.1 convert_reduce_fusion.2
  79.4 0.1 reshape.193
  79.5 356.0 %all-to-all-done.1 = bf16[32,1,64,4096]{3,2,1,0:T(8,128)(2,1)} async-done(((bf16[32,1,64,4096]{3,2,1,0:T(8,128)(2,1)}), bf16[32,1,64,4096]{3,2,1,0:T(8,128)(2,1)}, u32[]{:S(2)}, u32[]{:S(2)}) %all-to-all-start.1) | async-done | bytes 16777248 | tf_op jit(solution)/shard_map/all_to_all | solution.py:77
  435.5 22.5 %fusion.4 = (bf16[2048]{0:T(1024)(128)(2,1)S(1)}, f32[2048,768]{0,1:T(8,128)}) fusion(bf16[1,2048,768]{1,2,0:T(8,128)(2,1)} %copy.62, bf16[1,2048,768]{1,2,0:T(8,128)(2,1)} %copy.63, bf16[2048,4096]{1,0:T(8,128)(2,1)} %bitcast.10, bf16[1,768,4096]{2,1,0:T(8,128)(2,1)} %param.15), kind=kOutput, calls=%fused_computation.17 | convolution fusion | flops 12899055616 | bytes 35655680 | tf_op jit(solution)/shard_map/rd,fd->rf/dot_general | solution.py:8
  458.0 0.7 convert_element_type.124
  458.7 16.5 %all-to-all-start.3 = ((bf16[1,32,64]{2,0,1:T(2,128)(2,1)}), bf16[1,32,64]{2,0,1:T(2,128)(2,1)S(1)}, u32[]{:S(2)}, u32[]{:S(2)}) async-start(bf16[1,32,64]{2,0,1:T(2,128)(2,1)} %convert_element_type.124), calls=%async_computation.3 | async-start | bytes 32768 | tf_op jit(solution)/shard_map/all_to_all | solution.py:109
  475.2 29.5 %fusion.10 = f32[2048,4096]{1,0:T(8,128)} fusion(bf16[1,4096,768]{2,1,0:T(8,128)(2,1)} %param.13, f32[2048,768]{0,1:T(8,128)} %get-tuple-element.18, bf16[1,2048,768]{1,2,0:T(8,128)(2,1)} %copy.62, bf16[1,2048,768]{1,2,0:T(8,128)(2,1)} %copy.63, f32[2048]{0:T(1024)S(1)} %reshape.193), kind=kOutput, calls=%fused_computation.23 | convolution fusion | flops 12905349120 | bytes 52436992 | tf_op jit(solution)/shard_map/rf,df->rd/dot_general | solution.py:20
  504.7 27.9 %add_convert_fusion = bf16[2048,4096]{1,0:T(8,128)(2,1)} fusion(f32[2048,4096]{1,0:T(8,128)} %fusion.10, bf16[1,4096,768]{2,1,0:T(8,128)(2,1)} %param.14, f32[2048,768]{0,1:T(8,128)} %get-tuple-element.18, f32[2048]{0:T(1024)S(1)} %reshape.193, bf16[1,2048,768]{1,2,0:T(8,128)(2,1)} %copy.63), kind=kOutput, calls=%fused_computation.6 | convolution fusion | flops 12914262016 | bytes 66068480 | tf_op jit(solution)/shard_map/rf,df->rd/dot_general | solution.py:21
  532.6 0.0 copy-start.4
  532.6 6.1 all-to-all-start.2
  538.7 0.0 reduce-scatter.2.cloned.1.call-start
  539.5 0.1 convert_reduce_fusion.3
  539.6 290.8 %psum.7 = f32[32]{0:T(128)S(1)} all-reduce(f32[32]{0:T(128)S(1)} %convert_reduce_fusion.3), channel_id=1, replica_groups=mesh['seq'=8,'exp'=4] {'seq'}, use_global_device_ids=true, to_apply=%region_13.14 | all-reduce | flops 32 | bytes 256 | tf_op jit(solution)/shard_map/psum | solution.py:75
  830.4 0.1 reduce.2
  830.4 0.1 reshape.192
  830.5 6.8 gather_fusion.2
  837.3 0.1 reshape.197
  837.4 0.2 multiply_reduce_fusion
  837.6 0.1 subtract_divide_fusion
  837.8 0.1 multiply_reduce_fusion.1
  837.9 0.1 multiply_convert_fusion.2
  838.0 1.1 convolution_bitcast_fusion
  839.1 0.0 reduce-scatter.2.cloned.1.call-update
  839.1 0.1 reshape.198
  839.2 0.7 copy.67
  839.9 64.5 %all-to-all-done.2 = bf16[1,32,64,4096]{3,2,0,1:T(8,128)(2,1)} async-done(((bf16[1,32,64,4096]{3,2,0,1:T(8,128)(2,1)}), bf16[1,32,64,4096]{3,2,0,1:T(8,128)(2,1)}, u32[]{:S(2)}, u32[]{:S(2)}) %all-to-all-start.2) | async-done | bytes 16777248 | tf_op jit(solution)/shard_map/all_to_all | solution.py:102
  904.4 23.0 %gather_fusion.1 = bf16[1024,4096]{1,0:T(8,128)(2,1)} fusion(bf16[2048,4096]{1,0:T(8,128)(2,1)} %bitcast.19, s32[1024]{0:T(1024)S(1)} %broadcast_clamp_fusion), kind=kCustom, calls=%fused_computation.1 | custom fusion | bytes 16781312 | tf_op jit(solution)/shard_map/gather | solution.py:119
  927.4 9.1 convert_reduce_fusion
  936.5 1.4 fusion.15
  937.9 128.2 %reduce-scatter.2.cloned.1.call-done = f32[128,32]{0,1:T(8,128)} async-done(((f32[4096,32]{0,1:T(8,128)}), f32[128,32]{0,1:T(8,128)}) %reduce-scatter.2.cloned.1.call-update) | async-done | bytes 16400 | tf_op jit(solution)/shard_map/reduce_scatter | solution.py:138
  (31 shorter events, 0.3 us)
Async XLA Ops:
  7.2 12.1 %copy-start = (bf16[1,128,4096]{2,1,0:T(8,128)(2,1)S(1)}, bf16[1,128,4096]{2,1,0:T(8,128)(2,1)}, u32[]{:S(2)}) copy-start(bf16[1,128,4096]{2,1,0:T(8,128)(2,1)} %param.10) | copy-start | bytes 3145732
  20.7 0.6 copy-start.3
  20.8 7.8 copy-start.6
  20.8 7.8 copy-start.8
  21.5 27.5 %copy-start.1 = (bf16[1,128,4096]{2,1,0:T(8,128)(2,1)S(1)}, bf16[1,128,4096]{2,1,0:T(8,128)(2,1)}, u32[]{:S(2)}) copy-start(bf16[1,128,4096]{2,1,0:T(8,128)(2,1)} %param.11) | copy-start | bytes 3145732
  37.4 26.1 %all-to-all-start = ((bf16[32,1,64]{2,1,0:T(2,128)(2,1)}), bf16[32,1,64]{2,1,0:T(2,128)(2,1)S(1)}, u32[]{:S(2)}, u32[]{:S(2)}) async-start(bf16[32,1,64]{2,1,0:T(2,128)(2,1)} %reshape.249), calls=%async_computation | async-start | bytes 32768 | tf_op jit(solution)/shard_map/all_to_all | solution.py:84
  63.5 372.0 %all-to-all-start.1 = ((bf16[32,1,64,4096]{3,2,1,0:T(8,128)(2,1)}), bf16[32,1,64,4096]{3,2,1,0:T(8,128)(2,1)}, u32[]{:S(2)}, u32[]{:S(2)}) async-start(bf16[32,1,64,4096]{3,2,1,0:T(8,128)(2,1)} %bitcast.92), calls=%async_computation.1 | async-start | bytes 33554432 | tf_op jit(solution)/shard_map/all_to_all | solution.py:77
  458.7 73.9 %all-to-all-start.3 = ((bf16[1,32,64]{2,0,1:T(2,128)(2,1)}), bf16[1,32,64]{2,0,1:T(2,128)(2,1)S(1)}, u32[]{:S(2)}, u32[]{:S(2)}) async-start(bf16[1,32,64]{2,0,1:T(2,128)(2,1)} %convert_element_type.124), calls=%async_computation.3 | async-start | bytes 32768 | tf_op jit(solution)/shard_map/all_to_all | solution.py:109
  532.6 6.8 copy-start.5
  532.6 305.2 %copy-start.4 = (f32[128,32]{0,1:T(8,128)S(1)}, f32[128,32]{0,1:T(8,128)}, u32[]{:S(2)}) copy-start(f32[128,32]{0,1:T(8,128)} %copy-done.3) | copy-start | bytes 49156
  532.6 305.2 %copy-start.7 = (f32[128]{0:T(128)S(1)}, f32[128]{0:T(128)}, u32[]{:S(2)}) copy-start(f32[128]{0:T(128)} %copy-done.6) | copy-start | bytes 1540
  532.6 305.2 %copy-start.9 = (f32[128]{0:T(128)S(1)}, f32[128]{0:T(128)}, u32[]{:S(2)}) copy-start(f32[128]{0:T(128)} %copy-done.8) | copy-start | bytes 1540
  532.6 371.7 %all-to-all-start.2 = ((bf16[1,32,64,4096]{3,2,0,1:T(8,128)(2,1)}), bf16[1,32,64,4096]{3,2,0,1:T(8,128)(2,1)}, u32[]{:S(2)}, u32[]{:S(2)}) async-start(bf16[1,32,64,4096]{3,2,0,1:T(8,128)(2,1)} %bitcast.93), calls=%async_computation.2 | async-start | bytes 33554432 | tf_op jit(solution)/shard_map/all_to_all | solution.py:102
  538.7 527.4 %reduce-scatter.2.cloned.1.call-start = ((), (), s32[]{:S(2)}) async-start(), calls=%async_computation.5 | async-start | bytes 540672 | tf_op jit(solution)/shard_map/reduce_scatter | solution.py:138
  927.4 9.1 copy-start.2
Sparse Core Ops, SparseCore 0:
  839.3 226.7 reduce-scatter.1
where the time goes:
time: 1080 us; the launch traced here: 1070 us
  waiting for transfers between devices  549 us (51%)
  blocking collectives  291 us (27%)
  matrix products  83.9 us (8%)
  local copies, waits for them, and re-layouts  77.6 us (7%)
  starting transfers between devices  36.4 us (3%)
  other arithmetic  20.6 us (2%)
  between operations  15.3 us (1%)
    all_to_all x1, waiting for transfers between devices, shards(): lax.all_to_all(grad_slots.reshape(experts, 1, capacity, model_width), ('s...  356 us
    psum x1, blocking collectives, shards(): seq_counts = lax.psum(local_counts, 'seq')  291 us
    reduce_scatter x1, waiting for transfers between devices, shards(): lax.psum_scatter(jnp.einsum('td,te->de', inputs, logit_grad, preferred_el...  128 us
    all_to_all x1, waiting for transfers between devices, shards(): lax.all_to_all(back_rows.reshape(1, devices, capacity, model_width), ('se...  64.5 us
    dot_general x1, matrix products, expert_backward(): jnp.einsum('rf,df->rd', grad_first, w_gate, preferred_element_type=jnp.fl...  29.5 us
    dot_general x1, matrix products, expert_backward(): jnp.einsum('rf,df->rd', grad_second, w_up, preferred_element_type=jnp.flo...  27.9 us
    gather x1, local copies, waits for them, and re-layouts, shards(): returned_rows[slot_index].reshape(tok_rows, top_count, model_width)  23 us
    dot_general x1, matrix products, expert_backward(): jnp.einsum('rd,fd->rf', grad_rows, w_down, preferred_element_type=jnp.flo...  22.5 us
  transfers between devices with their start and end apart: 5, of which 3 were waited for; matrix products, arithmetic and copies ran while one was open for 12% of the time, Pallas kernels for 0%

commit v1 on v0

--- a/solution.py
+++ b/solution.py
@@ -2,6 +2,13 @@
 import jax.numpy as jnp
 from jax import lax
 from jax.sharding import PartitionSpec as P
+
+
+def stacked_exchange(x, axis, split, join):
+    size = lax.axis_size(axis)
+    blocks = jnp.stack(jnp.split(x, size, axis=split), axis=0)
+    blocks = lax.all_to_all(blocks, axis, split_axis=0, concat_axis=0)
+    return jnp.concatenate(blocks, axis=join)
 
 
 def expert_backward(grad_rows, gate_rows, w_gate, w_up, w_down, pre_gate, pre_up):
@@ -74,12 +81,8 @@
     local_counts = jnp.sum(chosen_count, axis=0)
     seq_counts = lax.psum(local_counts, "seq")
     recv_grad, recv_gate = (
-        lax.all_to_all(
-            grad_slots.reshape(experts, 1, capacity, model_width),
-            ("seq", "exp"),
-            split_axis=0,
-            concat_axis=1,
-            tiled=True,
+        stacked_exchange(
+            grad_slots.reshape(experts, 1, capacity, model_width), ("seq", "exp"), 0, 1
         ),
         lax.all_to_all(
             gate_slots.reshape(experts, 1, capacity),

time: 1080 us -> 1140 us (1.056)
  local copies, waits for them, and re-layouts: 77.6 us -> 138 us
    unnamed x25 -> x72, local copies, waits for them, and re-layouts: 11.6 us -> 70.4 us
  transfers between devices with their start and end apart: 5 -> 5, of which waited for: 3 -> 3; matrix products, arithmetic and copies ran while one was open for 12% -> 17% of each run, Pallas kernels for 0% -> 0%
where the time goes in v1:
time: 1140 us; the launch traced here: 1130 us
  waiting for transfers between devices  549 us (48%)
  blocking collectives  291 us (26%)
  local copies, waits for them, and re-layouts  138 us (12%)
  matrix products  83.9 us (7%)
  starting transfers between devices  36.4 us (3%)
  other arithmetic  20.6 us (2%)
  between operations  15.4 us (1%)
    all_to_all x1, waiting for transfers between devices, stacked_exchange(): blocks = lax.all_to_all(blocks, axis, split_axis=0, concat_axis=0)  356 us
    psum x1, blocking collectives, shards(): seq_counts = lax.psum(local_counts, 'seq')  291 us
    reduce_scatter x1, waiting for transfers between devices, shards(): lax.psum_scatter(jnp.einsum('td,te->de', inputs, logit_grad, preferred_el...  128 us
    unnamed x72, local copies, waits for them, and re-layouts  70.4 us
    all_to_all x1, waiting for transfers between devices, shards(): lax.all_to_all(back_rows.reshape(1, devices, capacity, model_width), ('se...  64.5 us
    dot_general x1, matrix products, expert_backward(): jnp.einsum('rf,df->rd', grad_first, w_gate, preferred_element_type=jnp.fl...  29.5 us
    dot_general x1, matrix products, expert_backward(): jnp.einsum('rf,df->rd', grad_second, w_up, preferred_element_type=jnp.flo...  27.9 us
    gather x1, local copies, waits for them, and re-layouts, shards(): returned_rows[slot_index].reshape(tok_rows, top_count, model_width)  23 us
  transfers between devices with their start and end apart: 5, of which 3 were waited for; matrix products, arithmetic and copies ran while one was open for 17% of the time, Pallas kernels for 0%

profile of v1, /device:TPU:0, one launch (start us, length us, event | category | flops | bytes accessed | tf_op | source)
XLA Modules:
  0.0 1134.0 jit_solution(14907982485932970042)
XLA Ops:
  7.2 0.9 copy.52
  8.2 0.7 broadcast_multiply_fusion
  8.9 0.7 fusion.71
  9.6 9.0 reduce-window.6
  19.3 1.4 fusion.79
  20.9 0.4 copy-done.7
  21.5 7.0 gather_fusion.3
  28.9 0.4 copy-done.14
  29.4 7.6 scatter_custom_fusion
  37.0 0.7 reshape.302
  37.7 7.3 all-to-all-start
  45.0 4.3 scatter_custom_fusion.1
  49.5 14.3 %gather_fusion = bf16[2048,4096]{1,0:T(8,128)(2,1)} fusion(bf16[129,4096]{1,0:T(8,128)(2,1)S(1)} %concatenate.3, s32[2048]{0:T(1024)S(1)} %fusion.65), kind=kCustom, calls=%fused_computation | custom fusion | bytes 33562624 | tf_op jit(solution)/shard_map/gather | solution.py:74
  63.8 1.9 fusion.56
  65.7 1.9 fusion.55
  67.6 1.9 fusion.54
  69.5 1.9 fusion.53
  71.4 1.9 fusion.52
  73.2 1.9 fusion.51
  75.1 1.9 fusion.50
  77.0 1.9 fusion.49
  78.9 1.9 fusion.48
  80.7 1.9 fusion.47
  82.6 1.9 fusion.46
  84.5 1.9 fusion.45
  86.4 1.9 fusion.44
  88.3 1.9 fusion.43
  90.2 1.9 fusion.42
  92.1 1.9 fusion.41
  93.9 1.9 fusion.40
  95.9 1.9 fusion.39
  97.8 1.9 fusion.38
  99.7 1.9 fusion.37
  101.5 1.9 fusion.36
  103.4 1.9 fusion.35
  105.3 1.9 fusion.34
  107.2 1.9 fusion.33
  109.1 1.9 fusion.32
  111.0 1.9 fusion.31
  112.9 1.9 fusion.30
  114.7 1.9 fusion.29
  116.6 1.9 fusion.28
  118.5 1.9 fusion.27
  120.4 1.9 fusion.26
  122.3 1.9 fusion.25
  124.1 6.4 all-to-all-start.1
  130.6 4.7 copy.60
  135.3 4.7 copy.59
  140.1 356.0 %all-to-all-done.1 = bf16[32,1,1,64,4096]{4,3,2,1,0:T(8,128)(2,1)} async-done(((bf16[32,1,1,64,4096]{4,3,2,1,0:T(8,128)(2,1)}), bf16[32,1,1,64,4096]{4,3,2,1,0:T(8,128)(2,1)}, u32[]{:S(2)}, u32[]{:S(2)}) %all-to-all-start.1) | async-done | bytes 16777248 | tf_op jit(solution)/shard_map/all_to_all | solution.py:10
  496.1 22.5 %fusion.4 = (bf16[2048]{0:T(1024)(128)(2,1)S(1)}, f32[2048,768]{0,1:T(8,128)}) fusion(bf16[1,2048,768]{1,2,0:T(8,128)(2,1)} %copy.59, bf16[1,2048,768]{1,2,0:T(8,128)(2,1)} %copy.60, bf16[2048,4096]{1,0:T(8,128)(2,1)} %bitcast.40, bf16[1,768,4096]{2,1,0:T(8,128)(2,1)} %param.15), kind=kOutput, calls=%fused_computation.17 | convolution fusion | flops 12899055616 | bytes 35655680 | tf_op jit(solution)/shard_map/rd,fd->rf/dot_general | solution.py:15
  518.7 0.7 convert_element_type.124
  519.4 16.5 %all-to-all-start.3 = ((bf16[1,32,64]{2,0,1:T(2,128)(2,1)}), bf16[1,32,64]{2,0,1:T(2,128)(2,1)S(1)}, u32[]{:S(2)}, u32[]{:S(2)}) async-start(bf16[1,32,64]{2,0,1:T(2,128)(2,1)} %convert_element_type.124), calls=%async_computation.3 | async-start | bytes 32768 | tf_op jit(solution)/shard_map/all_to_all | solution.py:112
  535.9 29.5 %fusion.10 = f32[2048,4096]{1,0:T(8,128)} fusion(bf16[1,4096,768]{2,1,0:T(8,128)(2,1)} %param.13, f32[2048,768]{0,1:T(8,128)} %get-tuple-element.18, bf16[1,2048,768]{1,2,0:T(8,128)(2,1)} %copy.59, bf16[1,2048,768]{1,2,0:T(8,128)(2,1)} %copy.60, f32[2048]{0:T(1024)S(1)} %reshape.246), kind=kOutput, calls=%fused_computation.23 | convolution fusion | flops 12905349120 | bytes 52436992 | tf_op jit(solution)/shard_map/rf,df->rd/dot_general | solution.py:27
  565.4 27.9 %add_convert_fusion = bf16[2048,4096]{1,0:T(8,128)(2,1)} fusion(f32[2048,4096]{1,0:T(8,128)} %fusion.10, bf16[1,4096,768]{2,1,0:T(8,128)(2,1)} %param.14, f32[2048,768]{0,1:T(8,128)} %get-tuple-element.18, f32[2048]{0:T(1024)S(1)} %reshape.246, bf16[1,2048,768]{1,2,0:T(8,128)(2,1)} %copy.60), kind=kOutput, calls=%fused_computation.6 | convolution fusion | flops 12914262016 | bytes 66068480 | tf_op jit(solution)/shard_map/rf,df->rd/dot_general | solution.py:28
  593.3 6.1 all-to-all-start.2
  600.3 290.8 %psum.7 = f32[32]{0:T(128)S(1)} all-reduce(f32[32]{0:T(128)S(1)} %convert_reduce_fusion.3), channel_id=1, replica_groups=mesh['seq'=8,'exp'=4] {'seq'}, use_global_device_ids=true, to_apply=%region_13.14 | all-reduce | flops 32 | bytes 256 | tf_op jit(solution)/shard_map/psum | solution.py:82
  891.2 6.8 gather_fusion.2
  898.7 1.1 convolution_bitcast_fusion
  900.0 0.7 copy.64
  900.6 64.5 %all-to-all-done.2 = bf16[1,32,64,4096]{3,2,0,1:T(8,128)(2,1)} async-done(((bf16[1,32,64,4096]{3,2,0,1:T(8,128)(2,1)}), bf16[1,32,64,4096]{3,2,0,1:T(8,128)(2,1)}, u32[]{:S(2)}, u32[]{:S(2)}) %all-to-all-start.2) | async-done | bytes 16777248 | tf_op jit(solution)/shard_map/all_to_all | solution.py:105
  965.1 23.0 %gather_fusion.1 = bf16[1024,4096]{1,0:T(8,128)(2,1)} fusion(bf16[2048,4096]{1,0:T(8,128)(2,1)} %bitcast.49, s32[1024]{0:T(1024)S(1)} %broadcast_clamp_fusion), kind=kCustom, calls=%fused_computation.1 | custom fusion | bytes 16781312 | tf_op jit(solution)/shard_map/gather | solution.py:122
  988.1 9.1 convert_reduce_fusion
  997.2 1.4 fusion.15
  998.6 128.3 %reduce-scatter.2.cloned.1.call-done = f32[128,32]{0,1:T(8,128)} async-done(((f32[4096,32]{0,1:T(8,128)}), f32[128,32]{0,1:T(8,128)}) %reduce-scatter.2.cloned.1.call-update) | async-done | bytes 16400 | tf_op jit(solution)/shard_map/reduce_scatter | solution.py:141
  (79 shorter events, 2.8 us)
Async XLA Ops:
  7.2 12.2 %copy-start = (bf16[1,128,4096]{2,1,0:T(8,128)(2,1)S(1)}, bf16[1,128,4096]{2,1,0:T(8,128)(2,1)}, u32[]{:S(2)}) copy-start(bf16[1,128,4096]{2,1,0:T(8,128)(2,1)} %param.10) | copy-start | bytes 3145732
  8.1 20.6 %copy-start.1 = (s32[1,128,8]{2,1,0:T(8,128)}, s32[1,128,8]{2,1,0:T(8,128)S(1)}, u32[]{:S(2)}) copy-start(s32[1,128,8]{2,1,0:T(8,128)S(1)} %copy.52) | copy-start | bytes 12292
  20.7 0.6 copy-start.7
  20.8 7.7 copy-start.12
  20.8 7.7 copy-start.16
  21.5 27.9 %copy-start.3 = (bf16[1,128,4096]{2,1,0:T(8,128)(2,1)S(1)}, bf16[1,128,4096]{2,1,0:T(8,128)(2,1)}, u32[]{:S(2)}) copy-start(bf16[1,128,4096]{2,1,0:T(8,128)(2,1)} %param.11) | copy-start | bytes 3145732
  28.6 20.8 %copy-start.5 = (f32[128,8]{1,0:T(8,128)}, f32[128,8]{1,0:T(8,128)S(1)}, u32[]{:S(2)}) copy-start(f32[128,8]{1,0:T(8,128)S(1)} %reshape.279) | copy-start | bytes 12292
  28.7 0.6 copy-start.14
  29.4 20.0 %copy-start.10 = (s32[1024,1]{0,1:T(1,128)}, s32[1024,1]{0,1:T(1,128)S(1)}, u32[]{:S(2)}) copy-start(s32[1024,1]{0,1:T(1,128)S(1)} %compare_select_fusion.1) | copy-start | bytes 12292
  37.7 86.4 %all-to-all-start = ((bf16[32,1,64]{2,1,0:T(2,128)(2,1)}), bf16[32,1,64]{2,1,0:T(2,128)(2,1)S(1)}, u32[]{:S(2)}, u32[]{:S(2)}) async-start(bf16[32,1,64]{2,1,0:T(2,128)(2,1)} %reshape.302), calls=%async_computation | async-start | bytes 32768 | tf_op jit(solution)/shard_map/all_to_all | solution.py:87
  124.1 372.0 %all-to-all-start.1 = ((bf16[32,1,1,64,4096]{4,3,2,1,0:T(8,128)(2,1)}), bf16[32,1,1,64,4096]{4,3,2,1,0:T(8,128)(2,1)}, u32[]{:S(2)}, u32[]{:S(2)}) async-start(bf16[32,1,1,64,4096]{4,3,2,1,0:T(8,128)(2,1)} %fusion.25), calls=%async_computation.1 | async-start | bytes 33554432 | tf_op jit(solution)/shard_map/all_to_all | solution.py:10
  519.4 73.9 %all-to-all-start.3 = ((bf16[1,32,64]{2,0,1:T(2,128)(2,1)}), bf16[1,32,64]{2,0,1:T(2,128)(2,1)S(1)}, u32[]{:S(2)}, u32[]{:S(2)}) async-start(bf16[1,32,64]{2,0,1:T(2,128)(2,1)} %convert_element_type.124), calls=%async_computation.3 | async-start | bytes 32768 | tf_op jit(solution)/shard_map/all_to_all | solution.py:112
  593.3 6.9 copy-start.9
  593.3 297.8 %copy-start.11 = (s32[1024,1]{0,1:T(1,128)S(1)}, s32[1024,1]{0,1:T(1,128)}, u32[]{:S(2)}) copy-start(s32[1024,1]{0,1:T(1,128)} %copy-done.10) | copy-start | bytes 12292
  593.3 304.8 %copy-start.2 = (s32[1,128,8]{2,1,0:T(8,128)S(1)}, s32[1,128,8]{2,1,0:T(8,128)}, u32[]{:S(2)}) copy-start(s32[1,128,8]{2,1,0:T(8,128)} %copy-done.1) | copy-start | bytes 12292
  593.3 304.8 %copy-start.6 = (f32[128,8]{1,0:T(8,128)S(1)}, f32[128,8]{1,0:T(8,128)}, u32[]{:S(2)}) copy-start(f32[128,8]{1,0:T(8,128)} %copy-done.5) | copy-start | bytes 12292
  593.3 304.8 %copy-start.15 = (f32[128]{0:T(128)S(1)}, f32[128]{0:T(128)}, u32[]{:S(2)}) copy-start(f32[128]{0:T(128)} %copy-done.14) | copy-start | bytes 1540
  593.3 305.2 %copy-start.8 = (f32[128,32]{0,1:T(8,128)S(1)}, f32[128,32]{0,1:T(8,128)}, u32[]{:S(2)}) copy-start(f32[128,32]{0,1:T(8,128)} %copy-done.7) | copy-start | bytes 49156
  593.3 305.2 %copy-start.13 = (f32[128]{0:T(128)S(1)}, f32[128]{0:T(128)}, u32[]{:S(2)}) copy-start(f32[128]{0:T(128)} %copy-done.12) | copy-start | bytes 1540
  593.3 305.2 %copy-start.17 = (f32[128]{0:T(128)S(1)}, f32[128]{0:T(128)}, u32[]{:S(2)}) copy-start(f32[128]{0:T(128)} %copy-done.16) | copy-start | bytes 1540
  593.3 371.7 %all-to-all-start.2 = ((bf16[1,32,64,4096]{3,2,0,1:T(8,128)(2,1)}), bf16[1,32,64,4096]{3,2,0,1:T(8,128)(2,1)}, u32[]{:S(2)}, u32[]{:S(2)}) async-start(bf16[1,32,64,4096]{3,2,0,1:T(8,128)(2,1)} %bitcast.217), calls=%async_computation.2 | async-start | bytes 33554432 | tf_op jit(solution)/shard_map/all_to_all | solution.py:105
  599.4 527.5 %reduce-scatter.2.cloned.1.call-start = ((), (), s32[]{:S(2)}) async-start(), calls=%async_computation.5 | async-start | bytes 540672 | tf_op jit(solution)/shard_map/reduce_scatter | solution.py:141
  965.1 32.1 %copy-start.4 = (bf16[4096,32]{0,1:T(8,128)(2,1)S(1)}, bf16[4096,32]{0,1:T(8,128)(2,1)}, u32[]{:S(2)}) copy-start(bf16[4096,32]{0,1:T(8,128)(2,1)} %param.12) | copy-start | bytes 786436
Sparse Core Ops, SparseCore 0:
  900.0 226.8 reduce-scatter.1
